TPU v7x, 32 devices: a whole 2x2x4 slice. The times are simulated.
32 devices in a mesh: root: 4 (over z), virt: 4 (over y, x), occ: 2 (over core).
Axes of the slice: x: 2, y: 2, z: 4, core: 2. Of those that a mesh axis runs over, the one named last changes fastest.
Arguments:
- trial_singles: bfloat16 [8, 96], P('root'), may hold values from -6 to 6
- trial_doubles: bfloat16 [8, 480, 9216], P('root', 'virt', 'occ'), may hold values from -6 to 6
- occ_fock: bfloat16 [96, 96], replicated, may hold values from -0.625 to 0.625
- virt_fock: bfloat16 [480, 480], replicated, may hold values from -0.25 to 0.25
- w_ovoo: bfloat16 [96, 480, 9216], P('occ', 'virt', 'root'), may hold values from -0.625 to 0.625
- w_ooov: bfloat16 [96, 480, 9216], P('occ', 'virt', 'root'), may hold values from -0.0029296875 to 0.0029296875
- converged: int32 [8], replicated, may hold values from 0 to 1, as said below
Outputs:
- sigma_doubles: bfloat16 [8, 480, 9216], P('root', 'virt', 'occ')
- sigma_singles: float32 [8, 96], P('root')
- subspace: float32 [8, 8], P('root')
Inputs may be any that keep to these rules, and one draw needn't show every extreme that they name: `converged`: exactly 4 roots are active (0). In every draw at least one aligned block of 2 roots has all its roots active; other blocks may have none.
All inputs are finite; a program needn't handle non-finite values.
Results may differ from a plain program's by a relative error of at most 0.0044.
Values may be sent and summed in bfloat16 or wider, within the bound.
A program may use at most 256 MiB of HBM per device.

v0:
```python
import math
import jax
import jax.numpy as jnp
from jax import lax
from jax.sharding import PartitionSpec as P


def flat_pairs(left, right):
    return lax.dot_general(
        left.reshape(left.shape[0], -1),
        right.reshape(right.shape[0], -1),
        (((1,), (1,)), ((), ())),
        preferred_element_type=jnp.float32,
    )


def local(trial_singles, trial_doubles, occ_fock, virt_fock, w_ovoo, w_ooov, converged):
    local_roots, virt_local, pair_local = trial_doubles.shape
    occ_count = occ_fock.shape[0]
    virt_count = virt_fock.shape[0]
    root_count = converged.shape[0]
    root_groups = lax.axis_size("root")
    occ_groups = lax.axis_size("occ")
    root_index = lax.axis_index("root")
    occ_index = lax.axis_index("occ")
    occ_half = occ_count // occ_groups
    block_pairs = occ_count * occ_count // root_groups
    own_start = occ_index * occ_half
    active = (1 - converged).astype(jnp.float32)
    own_active = lax.dynamic_slice_in_dim(active, root_index * local_roots, local_roots)
    singles_all = lax.all_gather(trial_singles, "root", axis=0, tiled=True)
    gathered = lax.all_gather(trial_doubles, "occ", axis=2, tiled=True)
    fock_cols = lax.dynamic_slice_in_dim(occ_fock, own_start, occ_half, 1)
    batch_rows = local_roots * virt_local
    stacked = gathered.reshape(batch_rows, occ_count, occ_count)
    first_term = jnp.einsum(
        "ki,bkj->bij", fock_cols, stacked, preferred_element_type=jnp.float32
    ).reshape(local_roots, virt_local, pair_local)
    own_rows = trial_doubles.reshape(batch_rows, occ_half, occ_count)
    second_term = jnp.einsum(
        "bik,kj->bij", own_rows, occ_fock, preferred_element_type=jnp.float32
    ).reshape(local_roots, virt_local, pair_local)
    doubles_block = lax.all_to_all(gathered, "root", split_axis=2, concat_axis=0, tiled=True)
    partial_coupling = flat_pairs(doubles_block, w_ooov)
    coupling_part = lax.dynamic_update_slice(
        jnp.zeros((root_count, occ_count), jnp.float32), partial_coupling, (jnp.int32(0), own_start)
    )
    coupling = lax.psum(coupling_part, ("root", "virt", "occ"))
    singles_fock = jnp.dot(singles_all, occ_fock, preferred_element_type=jnp.float32)
    singles_every = active[:, None] * (-singles_fock - 0.5 * coupling)
    sigma_singles = lax.dynamic_slice_in_dim(singles_every, root_index * local_roots, local_roots)
    singles_cols = lax.dynamic_slice_in_dim(singles_all, own_start, occ_half, 1)
    outer_part = (
        -jnp.dot(singles_cols, w_ovoo.reshape(occ_half, -1), preferred_element_type=jnp.float32)
    ).reshape(root_count, virt_local, block_pairs)
    product = jnp.einsum(
        "ac,ncp->nap",
        virt_fock,
        lax.all_to_all(trial_doubles, "virt", split_axis=2, concat_axis=1, tiled=True),
        preferred_element_type=jnp.float32,
    ).astype(jnp.bfloat16)
    vv_term = lax.all_to_all(product, "virt", split_axis=1, concat_axis=2, tiled=True)
    vv_value = vv_term.astype(jnp.float32)
    outer_own = lax.all_to_all(outer_part, "root", split_axis=0, concat_axis=2, tiled=True)
    outer_half = lax.psum_scatter(outer_own, "occ", scatter_dimension=2, tiled=True)
    summed = vv_value + outer_half - first_term - second_term
    sigma_doubles = (own_active[:, None, None] * summed).astype(jnp.bfloat16)
    trial_piece, sigma_piece = (
        lax.all_to_all(trial_doubles, "root", split_axis=2, concat_axis=0, tiled=True),
        lax.all_to_all(sigma_doubles, "root", split_axis=2, concat_axis=0, tiled=True),
    )
    doubles_part = lax.psum(flat_pairs(trial_piece, sigma_piece), ("root", "virt", "occ"))
    singles_part = jnp.dot(
        singles_all.astype(jnp.float32), singles_every.T, precision=lax.Precision.HIGHEST
    )
    whole_matrix = doubles_part / math.sqrt(
        occ_count * occ_count * virt_count
    ) + singles_part / math.sqrt(occ_count)
    subspace = lax.dynamic_slice_in_dim(whole_matrix, root_index * local_roots, local_roots, 0)
    return (sigma_doubles, sigma_singles, subspace)


def solution(mesh):
    placed = (
        P("root", None),
        P("root", "virt", "occ"),
        P(),
        P(),
        P("occ", "virt", "root"),
        P("occ", "virt", "root"),
        P(),
    )
    return jax.shard_map(
        local,
        mesh=mesh,
        in_specs=placed,
        out_specs=(P("root", "virt", "occ"), P("root", None), P("root", None)),
        check_vma=False,
    )
```

profile of v0, /device:TPU:0, one launch (start us, length us, event | category | flops | bytes accessed | tf_op | source)
XLA Modules:
  0.0 595.7 jit_solution(10986336026013833331)
XLA Ops:
  7.2 0.0 copy-start
  7.2 6.9 %copy.53 = bf16[2,120,4608]{1,0,2:T(2,128)(2,1)} copy(bf16[2,120,4608]{2,1,0:T(8,128)(2,1)} %param.8) | data formatting | bytes 4423680 | tf_op args[1]
  14.1 5.2 all-to-all-start
  19.3 24.4 %copy.79 = bf16[6,8,120,2304]{3,1,2,0:T(8,128)(2,1)} copy(bf16[6,8,120,2304]{3,2,1,0:T(8,128)(2,1)} %bitcast.88) | data formatting | bytes 53084160
  43.7 0.0 copy-done.4
  43.7 11.1 %all-gather = bf16[4,2,96]{2,1,0:T(2,128)(2,1)S(1)} all-gather(bf16[1,2,96]{2,1,0:T(2,128)(2,1)S(1)} %bitcast.102), channel_id=1, replica_groups=mesh['root'=4,'virt'=4,'occ'=2] {'root'}, dimensions={0}, use_global_device_ids=true | all-gather | bytes 1920 | tf_op jit(solution)/shard_map/all_gather | solution.py:31
  54.8 10.4 %convolution_negate_fusion = f32[8,276480]{1,0:T(8,128)S(1)} fusion(bf16[48,276480]{1,0:T(8,128)(2,1)} %bitcast.84, bf16[8,96]{1,0:T(8,128)(2,1)S(1)} %bitcast.99, s32[]{:T(128)S(6)} %select_n.5), kind=kOutput, calls=%fused_computation | convolution fusion | flops 214548480 | bytes 35390980 | tf_op jit(solution)/shard_map/dot_general | solution.py:54
  65.3 6.1 %copy.57 = f32[8,120,2304]{2,1,0:T(8,128)} copy(f32[8,120,2304]{2,0,1:T(8,128)S(1)} %bitcast.85) | data formatting | bytes 17694720 | tf_op jit(solution)/shard_map/reshape | solution.py:55
  71.4 0.0 all-to-all-done
  71.4 5.7 all-to-all-start.2
  77.1 0.0 all-gather.3.cloned.1.call-start
  77.2 0.7 all-gather.3.cloned.1.call-update
  77.8 4.4 copy.54
  82.2 0.0 copy-done
  82.2 2.9 fusion.4
  85.2 3.1 copy.55
  88.3 180.0 %all-to-all-done.2 = f32[8,120,2304]{2,1,0:T(8,128)} async-done(((f32[8,120,2304]{2,1,0:T(8,128)}), f32[8,120,2304]{2,1,0:T(8,128)}, u32[]{:S(2)}, u32[]{:S(2)}) %all-to-all-start.2) | async-done | bytes 8847392 | tf_op jit(solution)/shard_map/all_to_all | solution.py:64
  268.2 3.9 all-to-all-start.1
  272.1 0.0 all-reduce.4.cloned.1.call-start
  272.1 14.5 %copy.58 = f32[2,120,4,2304]{1,0,3,2:T(2,128)} copy(f32[2,120,4,2304]{3,1,0,2:T(8,128)} %bitcast.12) | data formatting | bytes 17694720 | tf_op jit(solution)/shard_map/all_to_all | solution.py:64
  286.6 0.0 all-reduce.4.cloned.1.call-update
  286.6 10.8 %all-to-all-done.1 = bf16[2,480,1152]{2,0,1:T(2,128)(2,1)S(1)} async-done(((bf16[2,480,1152]{2,0,1:T(2,128)(2,1)}), bf16[2,480,1152]{2,0,1:T(2,128)(2,1)S(1)}, u32[]{:S(2)}, u32[]{:S(2)}) %all-to-all-start.1) | async-done | bytes 2211872 | tf_op jit(solution)/shard_map/all_to_all | solution.py:62
  297.5 1.4 copy-done.2
  298.8 3.7 all-to-all-start.5
  302.5 0.0 all-gather.3.cloned.1.call-done
  302.6 12.7 %copy.65 = bf16[2,120,9216]{1,0,2:T(2,128)(2,1)} copy(bf16[2,120,9216]{2,1,0:T(8,128)(2,1)} %all-gather.3.cloned.1.call-done) | data formatting | bytes 8847360 | tf_op jit(solution)/shard_map/all_gather | solution.py:32
  315.3 40.6 %all-to-all-done.5 = bf16[2,120,4608]{1,0,2:T(2,128)(2,1)S(1)} async-done(((bf16[2,120,4608]{1,0,2:T(2,128)(2,1)}), bf16[2,120,4608]{1,0,2:T(2,128)(2,1)S(1)}, u32[]{:S(2)}, u32[]{:S(2)}) %all-to-all-start.5) | async-done | bytes 2211872 | tf_op jit(solution)/shard_map/all_to_all | solution.py:69
  356.0 5.1 all-to-all-start.3
  361.1 0.0 copy-start.3
  361.1 5.9 reshape.49
  367.0 0.0 copy-done.3
  367.0 4.7 fusion.11
  371.6 7.1 %reshape.50 = f32[2,120,4608]{1,0,2:T(2,128)} reshape(f32[240,48,96]{0,2,1:T(8,128)} %fusion.11) | data formatting | bytes 8847360 | tf_op jit(solution)/shard_map/reshape | solution.py:42
  378.8 0.0 copy-done.5
  378.8 0.1 dynamic_slice.15
  378.9 0.0 copy-done.6
  378.9 0.6 dynamic-slice
  380.1 8.9 %copy.56 = f32[2,4,120,1152]{2,0,3,1:T(2,128)} copy(bf16[2,4,120,1152]{3,0,2,1:T(2,128)(2,1)} %bitcast.95) | data formatting | bytes 6635520 | tf_op jit(solution)/shard_map/convert_element_type | solution.py:63
  389.0 9.5 %reshape.62 = bf16[240,96,96]{2,1,0:T(8,128)(2,1)} reshape(bf16[2,120,9216]{2,1,0:T(8,128)(2,1)} %all-gather.3.cloned.1.call-done) | data formatting | bytes 8847360 | tf_op jit(solution)/shard_map/reshape | solution.py:35
  398.6 9.2 %copy.61 = bf16[240,96,96]{0,1,2:T(8,128)(2,1)} copy(bf16[240,96,96]{2,1,0:T(8,128)(2,1)} %reshape.62) | data formatting | bytes 8847360 | tf_op jit(solution)/shard_map/reshape | solution.py:35
  407.8 3.2 convolution_bitcast_fusion
  411.0 4.8 copy.62
  415.9 7.1 %reshape.48 = f32[2,120,4608]{1,0,2:T(2,128)} reshape(f32[240,48,96]{0,2,1:T(8,128)} %copy.62) | data formatting | bytes 8847360 | tf_op jit(solution)/shard_map/reshape | solution.py:38
  423.0 10.2 %fusion.3 = bf16[2,120,4608]{1,0,2:T(2,128)(2,1)} fusion(f32[2,120,4608]{1,0,2:T(2,128)} %reshape.50, f32[2,120,4608]{1,0,2:T(2,128)} %reshape.48, f32[2,120,9216]{1,0,2:T(2,128)} %all-reduce.4.cloned.1.call-done, u32[]{:T(128)S(6)} %multiply.4, f32[2,4,120,1152]{2,0,3,1:T(2,128)} %copy.56, f32[2]{0:T(128)S(1)} %dynamic_slice.15), kind=kLoop, calls=%fused_computation.5 | loop fusion | flops 5529600 | bytes 19906572 | tf_op jit(solution)/shard_map/convert_element_type | solution.py:67
  433.2 31.7 %all-to-all-done.3 = bf16[2,120,9216]{1,0,2:T(2,128)(2,1)} async-done(((bf16[2,120,9216]{1,0,2:T(2,128)(2,1)}), bf16[2,120,9216]{1,0,2:T(2,128)(2,1)}, u32[]{:S(2)}, u32[]{:S(2)}) %all-to-all-start.3) | async-done | bytes 4423712 | tf_op jit(solution)/shard_map/all_to_all | solution.py:43
  464.9 4.7 all-to-all-start.4
  469.6 24.4 %copy.81 = bf16[6,8,120,2304]{3,1,2,0:T(8,128)(2,1)} copy(bf16[6,8,120,2304]{3,2,1,0:T(8,128)(2,1)} %bitcast.89) | data formatting | bytes 53084160
  494.0 4.3 copy.69
  498.3 1.9 copy.83
  500.2 12.3 %copy.66 = bf16[2,120,4,2304]{3,1,0,2:T(8,128)(2,1)} copy(bf16[2,120,4,2304]{1,0,3,2:T(2,128)(2,1)} %bitcast.17) | data formatting | bytes 8847360 | tf_op jit(solution)/shard_map/all_to_all | solution.py:43
  512.5 5.2 copy.80
  517.7 13.4 %fusion.17 = f32[8,48]{1,0:T(8,128)S(1)} fusion(bf16[8,276480]{1,0:T(8,128)(2,1)} %bitcast.87, bf16[48,276480]{1,0:T(8,128)(2,1)} %bitcast.83), kind=kOutput, calls=%fused_computation.27 | convolution fusion | flops 212336640 | bytes 30967296 | tf_op jit(solution)/shard_map/dot_general | solution.py:9
  531.0 0.2 dynamic_update_slice.3
  531.2 6.7 %copy.71 = bf16[2,120,4608]{2,1,0:T(8,128)(2,1)} copy(bf16[2,120,4608]{1,0,2:T(2,128)(2,1)} %fusion.3) | data formatting | bytes 4423680
  537.9 0.0 all-to-all-done.4
  537.9 6.8 %copy.67 = bf16[2,120,4,1152]{3,1,0,2:T(8,128)(2,1)} copy(bf16[2,120,4,1152]{1,0,3,2:T(2,128)(2,1)} %bitcast.19) | data formatting | bytes 4423680 | tf_op jit(solution)/shard_map/all_to_all | solution.py:70
  544.7 1.9 copy.82
  546.6 1.2 convolution_bitcast_fusion.1
  547.8 39.5 %all-reduce.1 = (f32[8,96]{1,0:T(8,128)S(1)}, f32[8,8]{0,1:T(8,128)S(1)}) all-reduce(f32[8,96]{1,0:T(8,128)S(1)} %dynamic_update_slice.3, f32[8,8]{0,1:T(8,128)S(1)} %convolution_bitcast_fusion.1), channel_id=1, replica_groups=mesh['root'=4,'virt'=4,'occ'=2] {'root','virt','occ'}, use_global_device_ids=true, to_apply=%region_1.0 | all-reduce | flops 832 | bytes 6656 | tf_op jit(solution)/shard_map/psum | solution.py:48
  587.3 0.1 fusion.8
  587.4 0.6 constant_dynamic-slice_fusion.1
  588.0 0.1 fusion.6
  588.2 0.1 constant_dynamic-slice_fusion
  588.2 0.7 copy.72
  (9 shorter events, 0.0 us)
Async XLA Ops:
  7.2 75.1 %copy-start = (bf16[480,480]{1,0:T(8,128)(2,1)S(1)}, bf16[480,480]{1,0:T(8,128)(2,1)}, u32[]{:S(2)}) copy-start(bf16[480,480]{1,0:T(8,128)(2,1)} %param.10) | copy-start | bytes 1382404
  14.1 57.3 %all-to-all-start = ((bf16[2,120,4608]{1,0,2:T(2,128)(2,1)}), bf16[2,120,4608]{1,0,2:T(2,128)(2,1)S(1)}, u32[]{:S(2)}, u32[]{:S(2)}) async-start(bf16[2,120,4608]{1,0,2:T(2,128)(2,1)} %copy.53), calls=%async_computation | async-start | bytes 4718592 | tf_op jit(solution)/shard_map/all_to_all | solution.py:59
  19.3 24.4 %copy-start.4 = (bf16[2,96]{1,0:T(2,128)(2,1)S(1)}, bf16[2,96]{1,0:T(2,128)(2,1)}, u32[]{:S(2)}) copy-start(bf16[2,96]{1,0:T(2,128)(2,1)} %param.7) | copy-start | bytes 1156
  71.4 196.8 %all-to-all-start.2 = ((f32[8,120,2304]{2,1,0:T(8,128)}), f32[8,120,2304]{2,1,0:T(8,128)}, u32[]{:S(2)}, u32[]{:S(2)}) async-start(f32[8,120,2304]{2,1,0:T(8,128)} %copy.57), calls=%async_computation.2 | async-start | bytes 17694720 | tf_op jit(solution)/shard_map/all_to_all | solution.py:64
  77.1 225.4 %all-gather.3.cloned.1.call-start = ((), (), s32[]{:S(2)}) async-start(), calls=%async_computation.6 | async-start | bytes 6635520 | tf_op jit(solution)/shard_map/all_gather | solution.py:32
  268.2 29.2 %all-to-all-start.1 = ((bf16[2,480,1152]{2,0,1:T(2,128)(2,1)}), bf16[2,480,1152]{2,0,1:T(2,128)(2,1)S(1)}, u32[]{:S(2)}, u32[]{:S(2)}) async-start(bf16[2,480,1152]{2,0,1:T(2,128)(2,1)} %copy.55), calls=%async_computation.1 | async-start | bytes 4423680 | tf_op jit(solution)/shard_map/all_to_all | solution.py:62
  272.1 150.9 %all-reduce.4.cloned.1.call-start = ((), (), s32[]{:S(2)}) async-start(), calls=%async_computation.7 | async-start | bytes 18874368
  297.5 1.4 copy-start.2
  298.8 57.1 %all-to-all-start.5 = ((bf16[2,120,4608]{1,0,2:T(2,128)(2,1)}), bf16[2,120,4608]{1,0,2:T(2,128)(2,1)S(1)}, u32[]{:S(2)}, u32[]{:S(2)}) async-start(bf16[2,120,4608]{1,0,2:T(2,128)(2,1)} %copy.53), calls=%async_computation.5 | async-start | bytes 4718592 | tf_op jit(solution)/shard_map/all_to_all | solution.py:69
  356.0 108.9 %all-to-all-start.3 = ((bf16[2,120,9216]{1,0,2:T(2,128)(2,1)}), bf16[2,120,9216]{1,0,2:T(2,128)(2,1)}, u32[]{:S(2)}, u32[]{:S(2)}) async-start(bf16[2,120,9216]{1,0,2:T(2,128)(2,1)} %copy.65), calls=%async_computation.3 | async-start | bytes 9437184 | tf_op jit(solution)/shard_map/all_to_all | solution.py:43
  361.1 5.9 copy-start.3
  371.6 7.2 %copy-start.5 = (s32[8]{0:T(128)S(1)}, s32[8]{0:T(128)}, u32[]{:S(2)}) copy-start(s32[8]{0:T(128)} %param.13) | copy-start | bytes 100
  371.6 7.2 %copy-start.6 = (u32[32]{0:T(128)S(1)}, u32[32]{0:T(128)}, u32[]{:S(2)}) copy-start(u32[32]{0:T(128)} %constant.35) | copy-start | bytes 388
  464.9 73.0 %all-to-all-start.4 = ((bf16[2,120,4608]{1,0,2:T(2,128)(2,1)}), bf16[2,120,4608]{1,0,2:T(2,128)(2,1)}, u32[]{:S(2)}, u32[]{:S(2)}) async-start(bf16[2,120,4608]{1,0,2:T(2,128)(2,1)} %fusion.3), calls=%async_computation.4 | async-start | bytes 4718592 | tf_op jit(solution)/shard_map/all_to_all | solution.py:70
  537.9 51.0 %copy-start.1 = (bf16[480,480]{1,0:T(8,128)(2,1)S(1)}, bf16[480,480]{1,0:T(8,128)(2,1)}, u32[]{:S(2)}) copy-start(bf16[480,480]{1,0:T(8,128)(2,1)} %param.10) | copy-start | bytes 1382404
Sparse Core Ops, SparseCore 0:
  79.5 15.8 all-gather.2
  286.7 40.7 all-reduce.3
where the time goes:
time: 599 us; the launch traced here: 596 us
  waiting for transfers between devices  264 us (44%)
  local copies, waits for them, and re-layouts  192 us (32%)
  blocking collectives  50.7 us (8%)
  matrix products  36.1 us (6%)
  starting transfers between devices  28.3 us (5%)
  between operations  14.8 us (2%)
  other arithmetic  10.2 us (2%)
    all_to_all x1, waiting for transfers between devices, local(): lax.all_to_all(outer_part, 'root', split_axis=0, concat_axis=2, tiled=True)  180 us
    unnamed x23, local copies, waits for them, and re-layouts  74 us
    all_to_all x1, waiting for transfers between devices, local(): lax.all_to_all(trial_doubles, 'root', split_axis=2, concat_axis=0, tiled=...  40.6 us
    psum x1, blocking collectives, local(): coupling = lax.psum(coupling_part, ('root', 'virt', 'occ'))  39.5 us
    all_to_all x1, waiting for transfers between devices, local(): lax.all_to_all(gathered, 'root', split_axis=2, concat_axis=0, tiled=True)  31.7 us
    reshape x2, local copies, waits for them, and re-layouts, local(): stacked = gathered.reshape(batch_rows, occ_count, occ_count)  18.8 us
    dot_general x2, matrix products, flat_pairs(): lax.dot_general(left.reshape(left.shape[0], -1), right.reshape(right.shap...  14.6 us
    all_to_all x1, local copies, waits for them, and re-layouts, local(): lax.all_to_all(outer_part, 'root', split_axis=0, concat_axis=2, tiled=True)  14.5 us
  transfers between devices with their start and end apart: 8, of which 4 were waited for; matrix products, arithmetic and copies ran while one was open for 37% of the time, Pallas kernels for 0%

commit v1 on v0

--- a/solution.py
+++ b/solution.py
@@ -15,6 +15,11 @@
 
 
 def local(trial_singles, trial_doubles, occ_fock, virt_fock, w_ovoo, w_ooov, converged):
+
+    def process_cubes(in_array, axis_tag):
+        passed = jnp.sum(jax.lax.all_gather(in_array, axis_tag), 0)
+        return passed
+
     local_roots, virt_local, pair_local = trial_doubles.shape
     occ_count = occ_fock.shape[0]
     virt_count = virt_fock.shape[0]
@@ -45,7 +50,7 @@
     coupling_part = lax.dynamic_update_slice(
         jnp.zeros((root_count, occ_count), jnp.float32), partial_coupling, (jnp.int32(0), own_start)
     )
-    coupling = lax.psum(coupling_part, ("root", "virt", "occ"))
+    coupling = process_cubes(coupling_part, ("root", "virt", "occ"))
     singles_fock = jnp.dot(singles_all, occ_fock, preferred_element_type=jnp.float32)
     singles_every = active[:, None] * (-singles_fock - 0.5 * coupling)
     sigma_singles = lax.dynamic_slice_in_dim(singles_every, root_index * local_roots, local_roots)

time: 599 us -> 637 us (1.063)
  blocking collectives: 50.7 us -> 87.8 us
    all_gather x0 -> x1, blocking collectives: none -> 39.8 us  [process_cubes(): passed = jnp.sum(jax.lax.all_gather(in_array, axis_tag), 0)]
  transfers between devices with their start and end apart: 8 -> 8, of which waited for: 4 -> 4; matrix products, arithmetic and copies ran while one was open for 37% -> 35% of each run, Pallas kernels for 0% -> 0%
where the time goes in v1:
time: 637 us; the launch traced here: 633 us
  waiting for transfers between devices  264 us (41%)
  local copies, waits for them, and re-layouts  192 us (30%)
  blocking collectives  87.8 us (14%)
  matrix products  36.1 us (6%)
  starting transfers between devices  28.4 us (4%)
  between operations  14.8 us (2%)
  other arithmetic  10.2 us (2%)
    all_to_all x1, waiting for transfers between devices, local(): lax.all_to_all(outer_part, 'root', split_axis=0, concat_axis=2, tiled=True)  180 us
    unnamed x23, local copies, waits for them, and re-layouts  74 us
    all_to_all x1, waiting for transfers between devices, local(): lax.all_to_all(trial_doubles, 'root', split_axis=2, concat_axis=0, tiled=...  40.7 us
    all_gather x1, blocking collectives, process_cubes(): passed = jnp.sum(jax.lax.all_gather(in_array, axis_tag), 0)  39.8 us
    psum x1, blocking collectives, local(): lax.psum(flat_pairs(trial_piece, sigma_piece), ('root', 'virt', 'occ'))  36.8 us
    all_to_all x1, waiting for transfers between devices, local(): lax.all_to_all(gathered, 'root', split_axis=2, concat_axis=0, tiled=True)  31.6 us
    reshape x2, local copies, waits for them, and re-layouts, local(): stacked = gathered.reshape(batch_rows, occ_count, occ_count)  18.8 us
    dot_general x2, matrix products, flat_pairs(): lax.dot_general(left.reshape(left.shape[0], -1), right.reshape(right.shap...  14.6 us
  transfers between devices with their start and end apart: 8, of which 4 were waited for; matrix products, arithmetic and copies ran while one was open for 35% of the time, Pallas kernels for 0%

profile of v1, /device:TPU:0, one launch (start us, length us, event | category | flops | bytes accessed | tf_op | source)
XLA Modules:
  0.0 633.0 jit_solution(2538199939010365140)
XLA Ops:
  7.2 0.0 copy-start
  7.2 6.9 %copy.53 = bf16[2,120,4608]{1,0,2:T(2,128)(2,1)} copy(bf16[2,120,4608]{2,1,0:T(8,128)(2,1)} %param.8) | data formatting | bytes 4423680 | tf_op args[1]
  14.1 5.2 all-to-all-start
  19.3 24.4 %copy.79 = bf16[6,8,120,2304]{3,1,2,0:T(8,128)(2,1)} copy(bf16[6,8,120,2304]{3,2,1,0:T(8,128)(2,1)} %bitcast.90) | data formatting | bytes 53084160
  43.7 0.0 copy-done.4
  43.7 11.1 %all-gather = bf16[4,2,96]{2,1,0:T(2,128)(2,1)S(1)} all-gather(bf16[1,2,96]{2,1,0:T(2,128)(2,1)S(1)} %bitcast.104), channel_id=1, replica_groups=mesh['root'=4,'virt'=4,'occ'=2] {'root'}, dimensions={0}, use_global_device_ids=true | all-gather | bytes 1920 | tf_op jit(solution)/shard_map/all_gather | solution.py:36
  54.8 10.4 %convolution_negate_fusion = f32[8,276480]{1,0:T(8,128)S(1)} fusion(bf16[48,276480]{1,0:T(8,128)(2,1)} %bitcast.86, bf16[8,96]{1,0:T(8,128)(2,1)S(1)} %bitcast.101, s32[]{:T(128)S(6)} %select_n.5), kind=kOutput, calls=%fused_computation | convolution fusion | flops 214548480 | bytes 35390980 | tf_op jit(solution)/shard_map/dot_general | solution.py:59
  65.3 6.1 copy.57
  71.4 0.0 all-to-all-done
  71.4 5.7 all-to-all-start.2
  77.1 0.0 all-gather.3.cloned.1.call-start
  77.2 0.7 all-gather.3.cloned.1.call-update
  77.9 4.4 copy.54
  82.3 0.0 copy-done
  82.3 2.9 fusion.4
  85.2 3.1 copy.55
  88.3 180.0 %all-to-all-done.2 = f32[8,120,2304]{2,1,0:T(8,128)} async-done(((f32[8,120,2304]{2,1,0:T(8,128)}), f32[8,120,2304]{2,1,0:T(8,128)}, u32[]{:S(2)}, u32[]{:S(2)}) %all-to-all-start.2) | async-done | bytes 8847392 | tf_op jit(solution)/shard_map/all_to_all | solution.py:69
  268.2 3.9 all-to-all-start.1
  272.1 0.0 all-reduce.3.cloned.1.call-start
  272.1 14.6 %copy.58 = f32[2,120,4,2304]{1,0,3,2:T(2,128)} copy(f32[2,120,4,2304]{3,1,0,2:T(8,128)} %bitcast.12) | data formatting | bytes 17694720 | tf_op jit(solution)/shard_map/all_to_all | solution.py:69
  286.7 0.0 all-reduce.3.cloned.1.call-update
  286.7 10.8 %all-to-all-done.1 = bf16[2,480,1152]{2,0,1:T(2,128)(2,1)S(1)} async-done(((bf16[2,480,1152]{2,0,1:T(2,128)(2,1)}), bf16[2,480,1152]{2,0,1:T(2,128)(2,1)S(1)}, u32[]{:S(2)}, u32[]{:S(2)}) %all-to-all-start.1) | async-done | bytes 2211872 | tf_op jit(solution)/shard_map/all_to_all | solution.py:67
  297.5 1.4 copy-done.2
  298.9 3.7 all-to-all-start.5
  302.6 0.0 all-gather.3.cloned.1.call-done
  302.6 12.7 %copy.65 = bf16[2,120,9216]{1,0,2:T(2,128)(2,1)} copy(bf16[2,120,9216]{2,1,0:T(8,128)(2,1)} %all-gather.3.cloned.1.call-done) | data formatting | bytes 8847360 | tf_op jit(solution)/shard_map/all_gather | solution.py:37
  315.3 40.7 %all-to-all-done.5 = bf16[2,120,4608]{1,0,2:T(2,128)(2,1)S(1)} async-done(((bf16[2,120,4608]{1,0,2:T(2,128)(2,1)}), bf16[2,120,4608]{1,0,2:T(2,128)(2,1)S(1)}, u32[]{:S(2)}, u32[]{:S(2)}) %all-to-all-start.5) | async-done | bytes 2211872 | tf_op jit(solution)/shard_map/all_to_all | solution.py:74
  356.0 5.1 all-to-all-start.3
  361.1 0.0 copy-start.3
  361.1 5.9 reshape.51
  367.0 0.0 copy-done.3
  367.0 4.7 fusion.11
  371.7 7.2 %reshape.52 = f32[2,120,4608]{1,0,2:T(2,128)} reshape(f32[240,48,96]{0,2,1:T(8,128)} %fusion.11) | data formatting | bytes 8847360 | tf_op jit(solution)/shard_map/reshape | solution.py:47
  378.9 0.0 copy-done.5
  378.9 0.1 dynamic_slice.15
  379.0 0.6 dynamic-slice
  380.2 8.9 %copy.56 = f32[2,4,120,1152]{2,0,3,1:T(2,128)} copy(bf16[2,4,120,1152]{3,0,2,1:T(2,128)(2,1)} %bitcast.97) | data formatting | bytes 6635520 | tf_op jit(solution)/shard_map/convert_element_type | solution.py:68
  389.1 9.5 %reshape.64 = bf16[240,96,96]{2,1,0:T(8,128)(2,1)} reshape(bf16[2,120,9216]{2,1,0:T(8,128)(2,1)} %all-gather.3.cloned.1.call-done) | data formatting | bytes 8847360 | tf_op jit(solution)/shard_map/reshape | solution.py:40
  398.7 9.2 %copy.61 = bf16[240,96,96]{0,1,2:T(8,128)(2,1)} copy(bf16[240,96,96]{2,1,0:T(8,128)(2,1)} %reshape.64) | data formatting | bytes 8847360 | tf_op jit(solution)/shard_map/reshape | solution.py:40
  407.9 3.2 convolution_bitcast_fusion
  411.1 4.8 copy.62
  416.0 7.1 %reshape.50 = f32[2,120,4608]{1,0,2:T(2,128)} reshape(f32[240,48,96]{0,2,1:T(8,128)} %copy.62) | data formatting | bytes 8847360 | tf_op jit(solution)/shard_map/reshape | solution.py:43
  423.1 10.2 %fusion.3 = bf16[2,120,4608]{1,0,2:T(2,128)(2,1)} fusion(f32[2,120,4608]{1,0,2:T(2,128)} %reshape.52, f32[2,120,4608]{1,0,2:T(2,128)} %reshape.50, f32[2,120,9216]{1,0,2:T(2,128)} %all-reduce.3.cloned.1.call-done, u32[]{:T(128)S(6)} %multiply.4, f32[2,4,120,1152]{2,0,3,1:T(2,128)} %copy.56, f32[2]{0:T(128)S(1)} %dynamic_slice.15), kind=kLoop, calls=%fused_computation.5 | loop fusion | flops 5529600 | bytes 19906572 | tf_op jit(solution)/shard_map/convert_element_type | solution.py:72
  433.3 31.6 %all-to-all-done.3 = bf16[2,120,9216]{1,0,2:T(2,128)(2,1)} async-done(((bf16[2,120,9216]{1,0,2:T(2,128)(2,1)}), bf16[2,120,9216]{1,0,2:T(2,128)(2,1)}, u32[]{:S(2)}, u32[]{:S(2)}) %all-to-all-start.3) | async-done | bytes 4423712 | tf_op jit(solution)/shard_map/all_to_all | solution.py:48
  464.9 4.7 all-to-all-start.4
  469.7 24.4 %copy.81 = bf16[6,8,120,2304]{3,1,2,0:T(8,128)(2,1)} copy(bf16[6,8,120,2304]{3,2,1,0:T(8,128)(2,1)} %bitcast.91) | data formatting | bytes 53084160
  494.1 4.3 copy.69
  498.4 1.9 copy.83
  500.3 12.3 %copy.66 = bf16[2,120,4,2304]{3,1,0,2:T(8,128)(2,1)} copy(bf16[2,120,4,2304]{1,0,3,2:T(2,128)(2,1)} %bitcast.17) | data formatting | bytes 8847360 | tf_op jit(solution)/shard_map/all_to_all | solution.py:48
  512.6 5.2 copy.80
  517.8 13.4 %convolution_bitcast_fusion.1 = f32[1,8,48]{2,1,0:T(8,128)S(1)} fusion(bf16[8,276480]{1,0:T(8,128)(2,1)} %bitcast.89, bf16[48,276480]{1,0:T(8,128)(2,1)} %bitcast.85), kind=kOutput, calls=%fused_computation.12 | convolution fusion | flops 212336640 | bytes 30967296 | tf_op jit(solution)/shard_map/dot_general | solution.py:9
  531.1 0.2 dynamic_update_slice.4
  531.3 39.8 %all_gather.15 = f32[32,8,96]{2,1,0:T(8,128)S(1)} all-gather(f32[1,8,96]{2,1,0:T(8,128)S(1)} %dynamic_update_slice.4), channel_id=1, replica_groups=mesh['root'=4,'virt'=4,'occ'=2] {'root','virt','occ'}, dimensions={0}, use_global_device_ids=true | all-gather | bytes 101376 | tf_op jit(solution)/shard_map/all_gather | solution.py:20
  571.2 0.1 fusion.8
  571.3 0.6 constant_dynamic-slice_fusion.1
  571.9 6.7 %copy.71 = bf16[2,120,4608]{2,1,0:T(8,128)(2,1)} copy(bf16[2,120,4608]{1,0,2:T(2,128)(2,1)} %fusion.3) | data formatting | bytes 4423680
  578.6 0.0 all-to-all-done.4
  578.6 6.8 %copy.67 = bf16[2,120,4,1152]{3,1,0,2:T(8,128)(2,1)} copy(bf16[2,120,4,1152]{1,0,3,2:T(2,128)(2,1)} %bitcast.20) | data formatting | bytes 4423680 | tf_op jit(solution)/shard_map/all_to_all | solution.py:75
  585.4 1.9 copy.82
  587.3 1.2 convolution_bitcast_fusion.2
  588.5 36.8 %psum.7 = f32[8,8]{0,1:T(8,128)S(1)} all-reduce(f32[8,8]{0,1:T(8,128)S(1)} %convolution_bitcast_fusion.2), channel_id=1, replica_groups=mesh['root'=4,'virt'=4,'occ'=2] {'root','virt','occ'}, use_global_device_ids=true, to_apply=%region_2.0 | all-reduce | flops 64 | bytes 512 | tf_op jit(solution)/shard_map/psum | solution.py:77
  625.3 0.1 fusion.6
  625.4 0.1 constant_dynamic-slice_fusion
  625.5 0.7 copy.72
  (11 shorter events, 0.1 us)
Async XLA Ops:
  7.2 75.1 %copy-start = (bf16[480,480]{1,0:T(8,128)(2,1)S(1)}, bf16[480,480]{1,0:T(8,128)(2,1)}, u32[]{:S(2)}) copy-start(bf16[480,480]{1,0:T(8,128)(2,1)} %param.10) | copy-start | bytes 1382404
  14.1 57.4 %all-to-all-start = ((bf16[2,120,4608]{1,0,2:T(2,128)(2,1)}), bf16[2,120,4608]{1,0,2:T(2,128)(2,1)S(1)}, u32[]{:S(2)}, u32[]{:S(2)}) async-start(bf16[2,120,4608]{1,0,2:T(2,128)(2,1)} %copy.53), calls=%async_computation | async-start | bytes 4718592 | tf_op jit(solution)/shard_map/all_to_all | solution.py:64
  19.3 24.4 %copy-start.4 = (bf16[2,96]{1,0:T(2,128)(2,1)S(1)}, bf16[2,96]{1,0:T(2,128)(2,1)}, u32[]{:S(2)}) copy-start(bf16[2,96]{1,0:T(2,128)(2,1)} %param.7) | copy-start | bytes 1156
  71.4 196.8 %all-to-all-start.2 = ((f32[8,120,2304]{2,1,0:T(8,128)}), f32[8,120,2304]{2,1,0:T(8,128)}, u32[]{:S(2)}, u32[]{:S(2)}) async-start(f32[8,120,2304]{2,1,0:T(8,128)} %copy.57), calls=%async_computation.2 | async-start | bytes 17694720 | tf_op jit(solution)/shard_map/all_to_all | solution.py:69
  77.1 225.4 %all-gather.3.cloned.1.call-start = ((), (), s32[]{:S(2)}) async-start(), calls=%async_computation.6 | async-start | bytes 6635520 | tf_op jit(solution)/shard_map/all_gather | solution.py:37
  268.2 29.2 %all-to-all-start.1 = ((bf16[2,480,1152]{2,0,1:T(2,128)(2,1)}), bf16[2,480,1152]{2,0,1:T(2,128)(2,1)S(1)}, u32[]{:S(2)}, u32[]{:S(2)}) async-start(bf16[2,480,1152]{2,0,1:T(2,128)(2,1)} %copy.55), calls=%async_computation.1 | async-start | bytes 4423680 | tf_op jit(solution)/shard_map/all_to_all | solution.py:67
  272.1 151.0 %all-reduce.3.cloned.1.call-start = ((), (), s32[]{:S(2)}) async-start(), calls=%async_computation.7 | async-start | bytes 18874368
  297.5 1.4 copy-start.2
  298.9 57.2 %all-to-all-start.5 = ((bf16[2,120,4608]{1,0,2:T(2,128)(2,1)}), bf16[2,120,4608]{1,0,2:T(2,128)(2,1)S(1)}, u32[]{:S(2)}, u32[]{:S(2)}) async-start(bf16[2,120,4608]{1,0,2:T(2,128)(2,1)} %copy.53), calls=%async_computation.5 | async-start | bytes 4718592 | tf_op jit(solution)/shard_map/all_to_all | solution.py:74
  356.0 108.9 %all-to-all-start.3 = ((bf16[2,120,9216]{1,0,2:T(2,128)(2,1)}), bf16[2,120,9216]{1,0,2:T(2,128)(2,1)}, u32[]{:S(2)}, u32[]{:S(2)}) async-start(bf16[2,120,9216]{1,0,2:T(2,128)(2,1)} %copy.65), calls=%async_computation.3 | async-start | bytes 9437184 | tf_op jit(solution)/shard_map/all_to_all | solution.py:48
  361.1 5.9 copy-start.3
  371.7 7.2 %copy-start.5 = (s32[8]{0:T(128)S(1)}, s32[8]{0:T(128)}, u32[]{:S(2)}) copy-start(s32[8]{0:T(128)} %param.13) | copy-start | bytes 100
  371.7 7.3 %copy-start.6 = (u32[32]{0:T(128)S(1)}, u32[32]{0:T(128)}, u32[]{:S(2)}) copy-start(u32[32]{0:T(128)} %constant.37) | copy-start | bytes 388
  464.9 113.6 %all-to-all-start.4 = ((bf16[2,120,4608]{1,0,2:T(2,128)(2,1)}), bf16[2,120,4608]{1,0,2:T(2,128)(2,1)}, u32[]{:S(2)}, u32[]{:S(2)}) async-start(bf16[2,120,4608]{1,0,2:T(2,128)(2,1)} %fusion.3), calls=%async_computation.4 | async-start | bytes 4718592 | tf_op jit(solution)/shard_map/all_to_all | solution.py:75
  578.6 47.6 %copy-start.1 = (bf16[480,480]{1,0:T(8,128)(2,1)S(1)}, bf16[480,480]{1,0:T(8,128)(2,1)}, u32[]{:S(2)}) copy-start(bf16[480,480]{1,0:T(8,128)(2,1)} %param.10) | copy-start | bytes 1382404
Sparse Core Ops, SparseCore 0:
  79.5 15.8 all-gather.2
  286.8 40.7 all-reduce.2
